TPU v7x, 32 devices: a whole 2x2x4 slice. The times are simulated.
32 devices in a mesh: dp: 4 (over y, x), vocab: 8 (over z, core).
Axes of the slice: x: 2, y: 2, z: 4, core: 2. Of those that a mesh axis runs over, the one named last changes fastest.
Arguments:
- hidden: bfloat16 [1024, 8192], P('dp'), may hold values from -14 to 14
- weight: bfloat16 [8192, 8192], P('dp', 'vocab'), may hold values from -1 to 1, as said below
- targets: int32 [1024], P('dp'), may hold values from 0 to 8191
- cotangent: float32 [1024], P('dp'), may hold values from 1 to 8
Outputs:
- loss: float32 [1024], P('dp')
- grad_hidden: bfloat16 [1024, 8192], P('vocab', 'dp')
- grad_weight: bfloat16 [8192, 8192], P('dp', 'vocab')
Inputs may be any that keep to these rules, and one draw needn't show every extreme that they name: `weight`: entries drawn with standard deviation 4 / sqrt(8192).
All inputs are finite; a program needn't handle non-finite values.
Results may differ from a plain program's by a relative error of at most 0.0047.
Values may be sent and summed in bfloat16 or wider, within the bound.
No kernel may reach another device: no remote copies, remote signals or barrier semaphores. Data moves between devices by JAX's collectives and lax.ppermute only.
A program may use at most 128 MiB of HBM per device.

v0:
```python
import jax
import jax.numpy as jnp
from jax import lax
from jax.sharding import PartitionSpec as P


def shards(hidden, weight, targets, cotangent):
    vocab_width = weight.shape[1]
    spread = lax.all_to_all(hidden, "dp", split_axis=1, concat_axis=0, tiled=True)
    vocab_first = lax.axis_index("vocab") * vocab_width
    columns = vocab_first + lax.iota(jnp.int32, vocab_width)
    onehot = (targets[:, None] == columns[None, :]).astype(jnp.float32)
    row_block = spread
    logits = lax.psum_scatter(
        jnp.dot(row_block, weight, preferred_element_type=jnp.float32),
        "dp",
        scatter_dimension=0,
        tiled=True,
    )
    local_max = jnp.max(logits, axis=1)
    local_pick = jnp.sum(logits * onehot, axis=1)
    row_max = lax.pmax(local_max, "vocab")
    shifted = jnp.exp(logits - row_max[:, None])
    sum_exp, picked = lax.psum((jnp.sum(shifted, axis=1), local_pick), "vocab")
    loss = row_max + jnp.log(sum_exp) - picked
    grad_logits = (cotangent[:, None] * (shifted / sum_exp[:, None] - onehot)).astype(jnp.bfloat16)
    all_grads = lax.all_gather(grad_logits, "dp", axis=0, tiled=True)
    grad_weight = lax.dot_general(
        spread, all_grads, (((0,), (0,)), ((), ())), preferred_element_type=jnp.float32
    ).astype(jnp.bfloat16)
    row_block = all_grads
    grad_hidden = lax.psum_scatter(
        lax.dot_general(
            row_block, weight, (((1,), (1,)), ((), ())), preferred_element_type=jnp.float32
        ),
        "vocab",
        scatter_dimension=0,
        tiled=True,
    ).astype(jnp.bfloat16)
    return (loss, grad_hidden, grad_weight)


def solution(mesh):
    in_specs = (P("dp", None), P("dp", "vocab"), P("dp"), P("dp"))
    out_specs = (P("dp"), P("vocab", "dp"), P("dp", "vocab"))
    return jax.shard_map(shards, mesh=mesh, in_specs=in_specs, out_specs=out_specs, check_vma=False)
```

profile of v0, /device:TPU:0, one launch (start us, length us, event | category | flops | bytes accessed | tf_op | source)
XLA Modules:
  0.0 314.0 jit_solution(2251081179240819122)
XLA Ops:
  7.2 0.0 reduce-scatter.3.cloned.1.call-start
  7.2 6.4 %copy.9 = bf16[256,8192]{0,1:T(8,128)(2,1)} copy(bf16[256,8192]{1,0:T(8,128)(2,1)} %param.4) | data formatting | bytes 8388608 | tf_op args[0]
  13.6 55.1 %all_to_all.19 = bf16[256,4,2048]{0,2,1:T(8,128)(2,1)} all-to-all(bf16[256,4,2048]{0,2,1:T(8,128)(2,1)} %bitcast.12), channel_id=1, replica_groups=mesh['dp'=4,'vocab'=8] {'dp'}, dimensions={1} | all-to-all | bytes 8388608 | tf_op jit(solution)/shard_map/all_to_all | solution.py:9
  68.7 6.2 %copy.10 = bf16[4,256,2048]{2,1,0:T(8,128)(2,1)} copy(bf16[4,256,2048]{1,2,0:T(8,128)(2,1)} %bitcast.11) | data formatting | bytes 8388608 | tf_op jit(solution)/shard_map/all_to_all | solution.py:9
  74.9 9.9 %fusion.5 = f32[1024,1024]{1,0:T(8,128)} fusion(bf16[1024,2048]{1,0:T(8,128)(2,1)} %bitcast.13, bf16[2048,1024]{1,0:T(8,128)(2,1)} %param.5), kind=kOutput, calls=%fused_computation.11 | convolution fusion | flops 4294967296 | bytes 12582912 | tf_op jit(solution)/shard_map/dot_general | solution.py:15
  84.7 0.0 copy-start
  84.8 0.0 copy-start.1
  84.8 0.0 reduce-scatter.3.cloned.1.call-update
  84.8 0.0 all-gather.2.cloned.1.call-start
  84.8 52.6 %reduce-scatter.3.cloned.1.call-done = f32[256,1024]{1,0:T(8,128)} async-done(((f32[1024,1024]{1,0:T(8,128)}), f32[256,1024]{1,0:T(8,128)}) %reduce-scatter.3.cloned.1.call-update) | async-done | bytes 1048592 | tf_op jit(solution)/shard_map/reduce_scatter | solution.py:14
  137.4 1.4 reduce_max.9
  138.8 16.2 %pmax.7 = f32[256]{0:T(256)S(1)} all-reduce(f32[256]{0:T(256)S(1)} %reduce_max.9), channel_id=1, replica_groups=mesh['dp'=4,'vocab'=8] {'vocab'}, use_global_device_ids=true, to_apply=%region_2.0 | all-reduce | flops 256 | bytes 2048 | tf_op jit(solution)/shard_map/pmax | solution.py:22
  155.0 0.0 copy-done
  155.0 1.6 fusion.4
  156.6 13.6 %all-reduce = (f32[256]{0:T(256)S(1)}, f32[256]{0:T(256)S(1)}) all-reduce(f32[256]{0:T(256)S(1)} %get-tuple-element.13, f32[256]{0:T(256)S(1)} %get-tuple-element.12), channel_id=1, replica_groups=mesh['dp'=4,'vocab'=8] {'vocab'}, use_global_device_ids=true, to_apply=%region_6.0 | all-reduce | flops 512 | bytes 4096 | tf_op jit(solution)/shard_map/psum | solution.py:24
  170.2 0.0 copy-done.1
  170.2 2.4 fusion.3
  172.6 0.0 all-gather.2.cloned.1.call-update
  172.6 0.0 reduce-scatter.5.cloned.1.call-start
  172.6 32.5 %all-gather.2.cloned.1.call-done = bf16[1024,1024]{1,0:T(8,128)(2,1)} async-done(((bf16[256,1024]{1,0:T(8,128)(2,1)}), bf16[1024,1024]{1,0:T(8,128)(2,1)}) %all-gather.2.cloned.1.call-update) | async-done | bytes 2097168 | tf_op jit(solution)/shard_map/all_gather | solution.py:27
  205.1 10.6 %fusion.6 = f32[1024,2048]{1,0:T(8,128)} fusion(bf16[1024,1024]{1,0:T(8,128)(2,1)} %all-gather.2.cloned.1.call-done, bf16[2048,1024]{1,0:T(8,128)(2,1)} %param.5), kind=kOutput, calls=%fused_computation.12 | convolution fusion | flops 4294967296 | bytes 14680064 | tf_op jit(solution)/shard_map/dot_general | solution.py:33
  215.7 0.0 copy-start.2
  215.7 0.0 reduce-scatter.5.cloned.1.call-update
  215.7 0.6 add_subtract_fusion
  216.3 1.0 copy-done.2
  217.3 8.3 %convert_bitcast_fusion = bf16[2048,1024]{0,1:T(8,128)(2,1)} fusion(bf16[1024,1024]{1,0:T(8,128)(2,1)S(1)} %copy-done.2, bf16[1024,2048]{1,0:T(8,128)(2,1)} %bitcast.14), kind=kOutput, calls=%fused_computation | convolution fusion | flops 4297064448 | bytes 10485760 | tf_op jit(solution)/shard_map/dot_general | solution.py:28
  225.6 6.4 %copy.11 = bf16[2048,1024]{1,0:T(8,128)(2,1)} copy(bf16[2048,1024]{0,1:T(8,128)(2,1)} %convert_bitcast_fusion) | data formatting | bytes 8388608
  232.0 73.4 %reduce-scatter.5.cloned.1.call-done = f32[128,2048]{1,0:T(8,128)} async-done(((f32[1024,2048]{1,0:T(8,128)}), f32[128,2048]{1,0:T(8,128)}) %reduce-scatter.5.cloned.1.call-update) | async-done | bytes 1048592 | tf_op jit(solution)/shard_map/reduce_scatter | solution.py:32
  305.4 2.1 convert_element_type.17
  (1 shorter events, 0.0 us)
Async XLA Ops:
  7.2 130.3 %reduce-scatter.3.cloned.1.call-start = ((), (), s32[]{:S(2)}) async-start(), calls=%async_computation.3 | async-start | bytes 5242880 | tf_op jit(solution)/shard_map/reduce_scatter | solution.py:14
  84.7 70.2 %copy-start = (s32[256]{0:T(256)S(1)}, s32[256]{0:T(256)}, u32[]{:S(2)}) copy-start(s32[256]{0:T(256)} %param.6) | copy-start | bytes 3076
  84.8 85.4 %copy-start.1 = (f32[256]{0:T(256)S(1)}, f32[256]{0:T(256)}, u32[]{:S(2)}) copy-start(f32[256]{0:T(256)} %param.7) | copy-start | bytes 3076
  84.8 120.4 %all-gather.2.cloned.1.call-start = ((), (), s32[]{:S(2)}) async-start(), calls=%async_computation.4 | async-start | bytes 2621440 | tf_op jit(solution)/shard_map/all_gather | solution.py:27
  172.6 132.9 %reduce-scatter.5.cloned.1.call-start = ((), (), s32[]{:S(2)}) async-start(), calls=%async_computation.5 | async-start | bytes 9437184 | tf_op jit(solution)/shard_map/reduce_scatter | solution.py:32
  215.7 1.6 copy-start.2
Sparse Core Ops, SparseCore 0:
  84.9 52.4 reduce-scatter.2
  172.7 32.3 all-gather.1
  215.9 89.5 reduce-scatter.4
where the time goes:
time: 315 us; the launch traced here: 314 us
  waiting for transfers between devices  159 us (50%)
  blocking collectives  84.9 us (27%)
  matrix products  28.7 us (9%)
  local copies, waits for them, and re-layouts  20 us (6%)
  between operations  13.8 us (4%)
  other arithmetic  8 us (3%)
    reduce_scatter x1, waiting for transfers between devices, shards(): lax.psum_scatter(lax.dot_general(row_block, weight, (((1,), (1,)), ((), (...  73.4 us
    all_to_all x1, blocking collectives, shards(): lax.all_to_all(hidden, 'dp', split_axis=1, concat_axis=0, tiled=True)  55.1 us
    reduce_scatter x1, waiting for transfers between devices, shards(): lax.psum_scatter(jnp.dot(row_block, weight, preferred_element_type=jnp.fl...  52.6 us
    all_gather x1, waiting for transfers between devices, shards(): all_grads = lax.all_gather(grad_logits, 'dp', axis=0, tiled=True)  32.5 us
    pmax x1, blocking collectives, shards(): row_max = lax.pmax(local_max, 'vocab')  16.2 us
    unnamed x8, local copies, waits for them, and re-layouts  13.8 us
    psum x1, blocking collectives, shards(): sum_exp, picked = lax.psum((jnp.sum(shifted, axis=1), local_pick), 'vocab')  13.6 us
    dot_general x1, matrix products, shards(): lax.dot_general(row_block, weight, (((1,), (1,)), ((), ())), preferred_el...  10.6 us
  transfers between devices with their start and end apart: 3, of which 3 were waited for; matrix products, arithmetic and copies ran while one was open for 5% of the time, Pallas kernels for 0%

commit v1 on v0

--- a/solution.py
+++ b/solution.py
@@ -5,8 +5,13 @@
 
 
 def shards(hidden, weight, targets, cotangent):
+
+    def mark_masks(vector, axis_name):
+        moved = jnp.stack(jnp.split(vector, lax.axis_size(axis_name), 1), axis=0)
+        return jnp.concatenate(lax.all_to_all(moved, axis_name, 0, 0), axis=0)
+
     vocab_width = weight.shape[1]
-    spread = lax.all_to_all(hidden, "dp", split_axis=1, concat_axis=0, tiled=True)
+    spread = mark_masks(hidden, "dp")
     vocab_first = lax.axis_index("vocab") * vocab_width
     columns = vocab_first + lax.iota(jnp.int32, vocab_width)
     onehot = (targets[:, None] == columns[None, :]).astype(jnp.float32)

time: 315 us -> 301 us (0.956)
  local copies, waits for them, and re-layouts: 20 us -> 5.74 us
  waiting for transfers between devices: 159 us -> 165 us
  matrix products: 28.7 us -> 24.9 us
    unnamed x8 -> x10, local copies, waits for them, and re-layouts: 13.8 us -> 2.98 us
    reduce_scatter x1, waiting for transfers between devices: 73.4 us -> 79.8 us  [shards(): lax.psum_scatter(lax.dot_general(row_block, weight, (((1,), (1,)), ((), (...]
    all_to_all x1 -> x0, local copies, waits for them, and re-layouts: 6.19 us -> none  [shards(): lax.all_to_all(hidden, 'dp', split_axis=1, concat_axis=0, tiled=True)]
    dot_general x1, matrix products: 9.88 us -> 6.01 us  [shards(): jnp.dot(row_block, weight, preferred_element_type=jnp.float32)]
  transfers between devices with their start and end apart: 3 -> 3, of which waited for: 3 -> 3; matrix products, arithmetic and copies ran while one was open for 5% -> 3% of each run, Pallas kernels for 0% -> 0%
where the time goes in v1:
time: 301 us
  waiting for transfers between devices  165 us (55%)
  blocking collectives  82.9 us (28%)
  matrix products  24.9 us (8%)
  between operations  13.8 us (5%)
  other arithmetic  8.57 us (3%)
  local copies, waits for them, and re-layouts  5.74 us (2%)
    reduce_scatter x1, waiting for transfers between devices, shards(): lax.psum_scatter(lax.dot_general(row_block, weight, (((1,), (1,)), ((), (...  79.8 us
    all_to_all x1, blocking collectives, mark_masks(): return jnp.concatenate(lax.all_to_all(moved, axis_name, 0, 0), axis=0)  53.1 us
    reduce_scatter x1, waiting for transfers between devices, shards(): lax.psum_scatter(jnp.dot(row_block, weight, preferred_element_type=jnp.fl...  52.4 us
    all_gather x1, waiting for transfers between devices, shards(): all_grads = lax.all_gather(grad_logits, 'dp', axis=0, tiled=True)  32.5 us
    pmax x1, blocking collectives, shards(): row_max = lax.pmax(local_max, 'vocab')  16.2 us
    psum x1, blocking collectives, shards(): sum_exp, picked = lax.psum((jnp.sum(shifted, axis=1), local_pick), 'vocab')  13.6 us
    dot_general x1, matrix products, shards(): lax.dot_general(row_block, weight, (((1,), (1,)), ((), ())), preferred_el...  10.6 us
    dot_general x1, matrix products, shards(): lax.dot_general(spread, all_grads, (((0,), (0,)), ((), ())), preferred_el...  8.3 us
  transfers between devices with their start and end apart: 3, of which 3 were waited for; matrix products, arithmetic and copies ran while one was open for 3% of the time, Pallas kernels for 0%

profile of v1, /device:TPU:0, one launch (start us, length us, event | category | flops | bytes accessed | tf_op | source)
XLA Modules:
  0.0 300.8 jit_solution(15217701985205269333)
XLA Ops:
  7.2 0.0 reduce-scatter.3.cloned.1.call-start
  7.2 2.8 slice_bitcast_fusion.3
  10.0 0.6 pad_maximum_fusion
  10.6 0.0 copy-start.3
  10.6 53.1 %all_to_all.5 = bf16[4,256,2048]{2,1,0:T(8,128)(2,1)S(1)} all-to-all(bf16[4,256,2048]{2,1,0:T(8,128)(2,1)S(1)} %pad_maximum_fusion), channel_id=1, replica_groups=mesh['dp'=4,'vocab'=8] {'dp'}, dimensions={0} | all-to-all | bytes 8388608 | tf_op jit(solution)/shard_map/all_to_all | solution.py:11
  63.7 0.0 copy-start
  63.7 2.0 copy-done
  65.6 0.0 copy-done.3
  65.6 6.0 %fusion.5 = f32[1024,1024]{1,0:T(8,128)} fusion(bf16[1024,2048]{1,0:T(8,128)(2,1)S(1)} %bitcast.15, bf16[2048,1024]{1,0:T(8,128)(2,1)S(1)} %copy-done.3), kind=kOutput, calls=%fused_computation.16 | convolution fusion | flops 4294967296 | bytes 12582912 | tf_op jit(solution)/shard_map/dot_general | solution.py:20
  71.7 0.0 copy-start.1
  71.7 0.0 copy-start.2
  71.7 0.0 reduce-scatter.3.cloned.1.call-update
  71.7 0.0 all-gather.2.cloned.1.call-start
  71.7 52.4 %reduce-scatter.3.cloned.1.call-done = f32[256,1024]{1,0:T(8,128)} async-done(((f32[1024,1024]{1,0:T(8,128)}), f32[256,1024]{1,0:T(8,128)}) %reduce-scatter.3.cloned.1.call-update) | async-done | bytes 1048592 | tf_op jit(solution)/shard_map/reduce_scatter | solution.py:19
  124.1 1.4 reduce_max.9
  125.5 16.2 %pmax.7 = f32[256]{0:T(256)S(1)} all-reduce(f32[256]{0:T(256)S(1)} %reduce_max.9), channel_id=1, replica_groups=mesh['dp'=4,'vocab'=8] {'vocab'}, use_global_device_ids=true, to_apply=%region_2.0 | all-reduce | flops 256 | bytes 2048 | tf_op jit(solution)/shard_map/pmax | solution.py:27
  141.7 0.0 copy-done.1
  141.7 1.6 fusion.4
  143.3 13.6 %all-reduce = (f32[256]{0:T(256)S(1)}, f32[256]{0:T(256)S(1)}) all-reduce(f32[256]{0:T(256)S(1)} %get-tuple-element.4, f32[256]{0:T(256)S(1)} %get-tuple-element.3), channel_id=1, replica_groups=mesh['dp'=4,'vocab'=8] {'vocab'}, use_global_device_ids=true, to_apply=%region_6.0 | all-reduce | flops 512 | bytes 4096 | tf_op jit(solution)/shard_map/psum | solution.py:29
  156.9 0.0 copy-done.2
  156.9 2.4 fusion.3
  159.3 0.0 all-gather.2.cloned.1.call-update
  159.3 0.0 reduce-scatter.5.cloned.1.call-start
  159.4 32.5 %all-gather.2.cloned.1.call-done = bf16[1024,1024]{1,0:T(8,128)(2,1)} async-done(((bf16[256,1024]{1,0:T(8,128)(2,1)}), bf16[1024,1024]{1,0:T(8,128)(2,1)}) %all-gather.2.cloned.1.call-update) | async-done | bytes 2097168 | tf_op jit(solution)/shard_map/all_gather | solution.py:32
  191.9 10.6 %fusion.6 = f32[1024,2048]{1,0:T(8,128)} fusion(bf16[1024,1024]{1,0:T(8,128)(2,1)} %all-gather.2.cloned.1.call-done, bf16[2048,1024]{1,0:T(8,128)(2,1)} %param.5), kind=kOutput, calls=%fused_computation.17 | convolution fusion | flops 4294967296 | bytes 14680064 | tf_op jit(solution)/shard_map/dot_general | solution.py:38
  202.4 0.0 copy-start.4
  202.4 0.0 reduce-scatter.5.cloned.1.call-update
  202.5 0.6 add_subtract_fusion
  203.0 1.0 copy-done.4
  204.0 8.3 %convolution_convert_fusion = bf16[2048,1024]{1,0:T(8,128)(2,1)} fusion(bf16[1024,2048]{1,0:T(8,128)(2,1)} %bitcast.16, bf16[1024,1024]{1,0:T(8,128)(2,1)S(1)} %copy-done.4), kind=kOutput, calls=%fused_computation.1 | convolution fusion | flops 4297064448 | bytes 10485760 | tf_op jit(solution)/shard_map/dot_general | solution.py:33
  212.3 79.8 %reduce-scatter.5.cloned.1.call-done = f32[128,2048]{1,0:T(8,128)} async-done(((f32[1024,2048]{1,0:T(8,128)}), f32[128,2048]{1,0:T(8,128)}) %reduce-scatter.5.cloned.1.call-update) | async-done | bytes 1048592 | tf_op jit(solution)/shard_map/reduce_scatter | solution.py:37
  292.1 2.1 convert_element_type.14
  (1 shorter events, 0.0 us)
Async XLA Ops:
  7.2 117.0 %reduce-scatter.3.cloned.1.call-start = ((), (), s32[]{:S(2)}) async-start(), calls=%async_computation.3 | async-start | bytes 5242880 | tf_op jit(solution)/shard_map/reduce_scatter | solution.py:19
  10.6 55.1 %copy-start.3 = (bf16[2048,1024]{1,0:T(8,128)(2,1)S(1)}, bf16[2048,1024]{1,0:T(8,128)(2,1)}, u32[]{:S(2)}) copy-start(bf16[2048,1024]{1,0:T(8,128)(2,1)} %param.5) | copy-start | bytes 12582916
  63.7 2.0 copy-start
  71.7 70.0 %copy-start.1 = (s32[256]{0:T(256)S(1)}, s32[256]{0:T(256)}, u32[]{:S(2)}) copy-start(s32[256]{0:T(256)} %param.6) | copy-start | bytes 3076
  71.7 85.2 %copy-start.2 = (f32[256]{0:T(256)S(1)}, f32[256]{0:T(256)}, u32[]{:S(2)}) copy-start(f32[256]{0:T(256)} %param.7) | copy-start | bytes 3076
  71.7 120.2 %all-gather.2.cloned.1.call-start = ((), (), s32[]{:S(2)}) async-start(), calls=%async_computation.4 | async-start | bytes 2621440 | tf_op jit(solution)/shard_map/all_gather | solution.py:32
  159.3 132.8 %reduce-scatter.5.cloned.1.call-start = ((), (), s32[]{:S(2)}) async-start(), calls=%async_computation.5 | async-start | bytes 9437184 | tf_op jit(solution)/shard_map/reduce_scatter | solution.py:37
  202.4 1.6 copy-start.4
Sparse Core Ops, SparseCore 0:
  71.8 52.2 reduce-scatter.2
  159.4 32.3 all-gather.1
  202.6 89.5 reduce-scatter.4
